TPU v7x, 512 devices: a whole 4x4x16 slice. The times are simulated.
512 devices in a mesh: row: 16 (over x_hi, y, core), col: 32 (over z, x_lo).
Axes of the slice: x: 4 (x_hi: 2, x_lo: 2; x = x_hi * 2 + x_lo), y: 4, z: 16, core: 2. Of those that a mesh axis runs over, the one named last changes fastest.
Arguments:
- tokens: bfloat16 [256, 16384], P('row', 'col'), may hold values from -6 to 6
- gate_weight: bfloat16 [16384, 26624], P('col', 'row'), may hold values from -0.046875 to 0.046875
- up_weight: bfloat16 [16384, 26624], P('col', 'row'), may hold values from -0.046875 to 0.046875
Outputs:
- hidden: bfloat16 [256, 26624], P(None, 'row')
All inputs are finite; a program needn't handle non-finite values.
Results may differ from a plain program's by a relative error of at most 0.001.
Values may be sent and summed in bfloat16 or wider, within the bound.
A program may use at most 64 MiB of HBM per device.

v0:
```python
import jax
import jax.numpy as jnp
from jax import lax
from jax.sharding import Mesh
from jax.sharding import PartitionSpec as P

COL = ("col_0", "col_1")


def laid_out(pieces, dim):
    pieces = jnp.moveaxis(pieces, 0, dim)
    lengths = pieces.shape
    return pieces.reshape(*lengths[:dim], lengths[dim] * lengths[dim + 1], *lengths[dim + 2 :])


def copy_for_each(value, axis):
    devices = lax.axis_size(axis)
    return lax.all_to_all(
        jnp.broadcast_to(value[None], (devices, *value.shape)), axis, 0, 0, tiled=True
    )


def gather_directly(value, axis, dim):
    return laid_out(copy_for_each(value, axis), dim)


def summed_rows(value, axes, dim):
    if not axes:
        return value
    nearer = lax.psum_scatter(value, axes[0], scatter_dimension=dim, tiled=True)
    return summed_rows(nearer, axes[1:], dim)


def gathered_by_axis(value, axes, dim):
    if not axes:
        return value
    nearer = lax.all_gather(value, axes[-1], axis=dim, tiled=True)
    return gathered_by_axis(nearer, axes[:-1], dim)


def local(tokens, gate_weight, up_weight):
    columns = gate_weight.shape[1]
    block_rows = gather_directly(tokens, "row", 0)
    gate_term = jnp.dot(block_rows, gate_weight, preferred_element_type=jnp.float32)
    up_term = jnp.dot(block_rows, up_weight, preferred_element_type=jnp.float32)
    partial_value = jnp.concatenate([gate_term, up_term], axis=1)
    shared = summed_rows(partial_value, COL, 0)
    gated = (jax.nn.silu(shared[:, :columns]) * shared[:, columns:]).astype(jnp.bfloat16)
    hidden = gathered_by_axis(gated, COL, 0)
    return hidden


def solution(mesh):
    split = Mesh(mesh.devices.reshape(mesh.shape["row"], 16, 2), ("row", "col_0", "col_1"))
    return jax.shard_map(
        local,
        mesh=split,
        in_specs=(P("row", COL), P(COL, "row"), P(COL, "row")),
        out_specs=P(None, "row"),
        check_vma=False,
    )
```

profile of v0, /device:TPU:16, one launch (start us, length us, event | category | flops | bytes accessed | tf_op | source)
XLA Modules:
  0.0 176.7 jit_solution(9003333131844445725)
XLA Ops:
  6.5 0.0 copy-start
  6.5 0.0 reduce-scatter.3.cloned.1.call-start
  6.5 0.9 broadcast_in_dim.2
  7.4 14.5 %all_to_all.5 = bf16[16,16,512]{2,1,0:T(8,128)(2,1)S(1)} all-to-all(bf16[16,16,512]{2,1,0:T(8,128)(2,1)S(1)} %broadcast_in_dim.2), channel_id=1, replica_groups=mesh['row'=16,'col_0'=16,'col_1'=2] {'row'}, dimensions={0} | all-to-all | bytes 524288 | tf_op jit(solution)/shard_map/all_to_all | solution.py:18
  21.9 0.0 copy-done
  21.9 0.0 copy-start.1
  21.9 0.6 fusion.2
  22.5 0.8 copy-done.1
  23.3 0.6 fusion.1
  24.0 2.0 %pad_maximum_fusion = f32[256,3328]{1,0:T(8,128)} fusion(f32[256,1664]{1,0:T(8,128)S(1)} %fusion.2, f32[256,1664]{1,0:T(8,128)S(1)} %fusion.1), kind=kLoop, calls=%fused_computation | loop fusion | flops 851968 | bytes 6815744 | tf_op jit(solution)/shard_map/concatenate | solution.py:46
  25.9 0.0 reduce-scatter.3.cloned.1.call-update
  26.0 0.0 reduce-scatter.5.cloned.1.call-start
  26.0 80.3 %reduce-scatter.3.cloned.1.call-done = f32[16,3328]{1,0:T(8,128)} async-done(((f32[256,3328]{1,0:T(8,128)}), f32[16,3328]{1,0:T(8,128)}) %reduce-scatter.3.cloned.1.call-update) | async-done | bytes 213008 | tf_op jit(solution)/shard_map/reduce_scatter | solution.py:30
  106.3 0.0 reduce-scatter.5.cloned.1.call-update
  106.3 21.6 %reduce-scatter.5.cloned.1.call-done = f32[8,3328]{1,0:T(8,128)} async-done(((f32[16,3328]{1,0:T(8,128)}), f32[8,3328]{1,0:T(8,128)}) %reduce-scatter.5.cloned.1.call-update) | async-done | bytes 106512 | tf_op jit(solution)/shard_map/reduce_scatter | solution.py:30
  127.9 0.9 fusion
  128.8 4.5 %all_gather.6 = bf16[16,1664]{1,0:T(8,128)(2,1)S(1)} all-gather(bf16[8,1664]{1,0:T(8,128)(2,1)S(1)} %fusion), channel_id=1, replica_groups=mesh['row'=16,'col_0'=16,'col_1'=2] {'col_1'}, dimensions={0}, use_global_device_ids=true | all-gather | bytes 79872 | tf_op jit(solution)/shard_map/all_gather | solution.py:37
  133.3 35.7 %all_gather.7 = bf16[256,1664]{1,0:T(8,128)(2,1)S(1)} all-gather(bf16[16,1664]{1,0:T(8,128)(2,1)S(1)} %all_gather.6), channel_id=1, replica_groups=mesh['row'=16,'col_0'=16,'col_1'=2] {'col_0'}, dimensions={0}, use_global_device_ids=true | all-gather | bytes 905216 | tf_op jit(solution)/shard_map/all_gather | solution.py:37
  169.0 0.9 copy.5
Async XLA Ops:
  6.5 15.3 %copy-start = (bf16[512,1664]{1,0:T(8,128)(2,1)S(1)}, bf16[512,1664]{1,0:T(8,128)(2,1)}, u32[]{:S(2)}) copy-start(bf16[512,1664]{1,0:T(8,128)(2,1)} %param.5) | copy-start | bytes 5111812
  6.5 99.8 %reduce-scatter.3.cloned.1.call-start = ((), (), s32[]{:S(2)}) async-start(), calls=%async_computation.3 | async-start | bytes 3620864 | tf_op jit(solution)/shard_map/reduce_scatter | solution.py:30
  21.9 1.5 copy-start.1
  26.0 102.0 %reduce-scatter.5.cloned.1.call-start = ((), (), s32[]{:S(2)}) async-start(), calls=%async_computation.4 | async-start | bytes 319488 | tf_op jit(solution)/shard_map/reduce_scatter | solution.py:30
Sparse Core Ops, SparseCore 0:
  26.1 80.1 reduce-scatter.2
  109.1 18.8 reduce-scatter.4
where the time goes:
time: 177 us
  waiting for transfers between devices  102 us (58%)
  blocking collectives  54.7 us (31%)
  between operations  13.4 us (8%)
  other arithmetic  2.81 us (2%)
  local copies, waits for them, and re-layouts  2.57 us (1%)
    reduce_scatter x2, waiting for transfers between devices, summed_rows(): nearer = lax.psum_scatter(value, axes[0], scatter_dimension=dim, tiled=True)  102 us
    all_gather x2, blocking collectives, gathered_by_axis(): nearer = lax.all_gather(value, axes[-1], axis=dim, tiled=True)  40.2 us
    all_to_all x1, blocking collectives, copy_for_each(): lax.all_to_all(jnp.broadcast_to(value[None], (devices, *value.shape)), ax...  14.5 us
  transfers between devices with their start and end apart: 2, of which 2 were waited for; matrix products, arithmetic and copies ran while one was open for 0% of the time, Pallas kernels for 0%

commit v1 on v0

v1 whole, which is shorter than its diff:
```python
import functools

import jax
import jax.numpy as jnp
from jax import lax
from jax.experimental import pallas as pl
from jax.experimental.pallas import tpu as pltpu
from jax.sharding import PartitionSpec as P

LANE = 128
B_TILES = (3, 2)
A_TILES = (4, 4)
STRIDE = 2


def kernel(nz, ny, nx, widths, n_b, tok_hbm, gate_hbm, up_hbm, out_hbm, *scratch):
    scratch = list(scratch)
    take = scratch.pop
    tok, wg, wu, hid = take(0), take(0), take(0), take(0)
    n_s = len(widths)
    part = [take(0) for _ in range(n_s)]
    slot = [take(0) for _ in range(n_s)]
    extra = [take(0) for _ in range(n_s)]
    total = [take(0) for _ in range(n_b)]
    load_sem, tok_send, tok_recv, pass_send, pass_recv = [take(0) for _ in range(5)]
    rs_send, rs_recv, x_send, x_recv = [take(0) for _ in range(4)]
    ag_send, ag_recv, agx_send, agx_recv, out_sem = [take(0) for _ in range(5)]

    row, col = lax.axis_index("row"), lax.axis_index("col")
    core = lax.rem(row, 2)
    y = lax.rem(row // 2, ny)
    xh = row // (2 * ny)
    z = col // 2
    xl = lax.rem(col, 2)
    other = 1 - xl
    sign = (1 - 2 * core, 2 * core - 1)
    hops = (nz // 2, nz - 1 - nz // 2)

    def at_z(d, t):
        return lax.rem(z + sign[d] * t + 2 * nz, nz)

    def z_id(d, t):
        return {"col": at_z(d, t) * 2 + xl}

    def row_of(dx, dy):
        return (lax.rem(xh + dx + nx, nx) * ny + lax.rem(y + dy + ny, ny)) * 2 + core

    x_id = {"col": z * 2 + other}
    partner = {"row": row + 1 - 2 * core}

    def remote(src, dst, send, recv, device):
        return pltpu.make_async_remote_copy(
            src_ref=src, dst_ref=dst, send_sem=send, recv_sem=recv,
            device_id=device, device_id_type=pl.DeviceIdType.MESH,
        )

    loads = [
        pltpu.make_async_copy(tok_hbm, tok.at[row], load_sem.at[0]),
        pltpu.make_async_copy(gate_hbm, wg, load_sem.at[1]),
        pltpu.make_async_copy(up_hbm, wu, load_sem.at[2]),
    ]
    for copy in loads:
        copy.start()

    offsets = [(dx, dy) for dx in range(nx) for dy in range(ny) if dx or dy]
    peers = [{"row": row_of(dx, dy)} for dx, dy in offsets]
    greet = peers + [partner, x_id]
    near = sorted({(d, t) for d in (0, 1) for t in range(1, STRIDE + 1)})
    greet += [z_id(d, t) for d, t in near]
    barrier = pltpu.get_barrier_semaphore()
    for device in greet:
        pl.semaphore_signal(barrier, inc=1, device_id=device, device_id_type=pl.DeviceIdType.MESH)
    pl.semaphore_wait(barrier, len(greet))

    loads[0].wait()
    started = []

    def go(copy):
        copy.start()
        started.append(copy)

    for o, device in reversed(list(enumerate(peers))):
        go(remote(tok.at[row], tok.at[row], tok_send.at[o], tok_recv.at[o], device))
    go(remote(tok.at[row], tok.at[row], pass_send.at[len(peers)], pass_recv.at[len(peers)], partner))
    for o, (dx, dy) in enumerate(offsets):
        src = row_of(-dx, -dy)
        remote(tok.at[src], tok.at[src], tok_send.at[o], tok_recv.at[o], peers[o]).wait_recv()
        go(remote(tok.at[src], tok.at[src], pass_send.at[o], pass_recv.at[o], partner))
    flip = 1 - 2 * core
    remote(tok.at[row], tok.at[row + flip], pass_send.at[len(peers)], pass_recv.at[len(peers)], partner).wait_recv()
    for o, (dx, dy) in enumerate(offsets):
        src = row_of(-dx, -dy) + flip
        remote(tok.at[src], tok.at[src], pass_send.at[o], pass_recv.at[o], partner).wait_recv()
    loads[1].wait()
    loads[2].wait()
    n_rows, rows_each, depth = tok.shape
    x = tok[...].reshape(n_rows * rows_each, depth)

    starts = [sum(widths[:i]) for i in range(n_s)]

    def multiply(i):
        w = widths[i]
        for half, ref in enumerate((wg, wu)):
            y_ = jnp.dot(x, ref[:, starts[i] : starts[i] + w], preferred_element_type=jnp.float32)
            part[i][:, :, :, half * w : (half + 1) * w] = y_.reshape(nz, 2, 8, w)

    order = [(d, t) for t in range(hops[0], 0, -1) for d in (0, 1) if t <= hops[d]] + [(0, 0)]
    place = {key: n for n, key in enumerate(order)}

    def index(d, t):
        return d * hops[0] + t - 1

    def rs(i, d, t, src):
        n = index(d, t)
        return remote(src, slot[i].at[n], rs_send.at[i, n], rs_recv.at[i, n], z_id(d, 1))

    def xs(i, n):
        d, t = order[n]
        return remote(part[i].at[at_z(d, t), other], extra[i].at[n], x_send.at[i, n], x_recv.at[i, n], x_id)

    def own(i, d, t):
        return part[i].at[at_z(d, t)] if i < n_b else part[i].at[at_z(d, t), xl]

    def step(i, d, t):
        ref = own(i, d, t)
        if i >= n_b:
            n = place[d, t]
            xs(i, n).wait_recv()
            ref[...] = ref[...] + extra[i][n]
        if t < hops[d]:
            n = index(d, t + 1)
            rs(i, d, t + 1, slot[i].at[n]).wait_recv()
            slot[i][n] = slot[i][n] + ref[...]
            ref = slot[i].at[n]
        go(rs(i, d, t, ref))

    todo = [(t, d) for t in range(hops[0], 0, -1) for d in (0, 1) if t <= hops[d]]
    for i in range(n_s):
        multiply(i)
        if i < n_b:
            for d in (0, 1):
                step(i, d, hops[d])
        else:
            for n in range(len(order)):
                go(xs(i, n))
    for t in range(hops[0], 0, -1):
        for i in range(n_s):
            for d in (0, 1):
                if t > hops[d] or (i < n_b and t == hops[d]):
                    continue
                step(i, d, t)

    def arrived(i):
        if hops[1]:
            ends = (0, 1)
        else:
            ends = (0,)
        for d in ends:
            rs(i, d, 1, slot[i].at[index(d, 1)]).wait_recv()
        value = slot[i][index(0, 1)]
        if hops[1]:
            value = value + slot[i][index(1, 1)]
        return value + own(i, 0, 0)[...]

    def finish(i, value):
        w = widths[i]
        gate, up = value[:, :w], value[:, w:]
        hid[z, xl, :, starts[i] : starts[i] + w] = (gate / (1.0 + jnp.exp(-gate)) * up).astype(jnp.bfloat16)

    for i in range(n_b):
        total[i][...] = arrived(i)
        go(remote(total[i].at[other], extra[i], x_send.at[i, 0], x_recv.at[i, 0], x_id))
    for i in range(n_b, n_s):
        n = place[0, 0]
        xs(i, n).wait_recv()
        finish(i, arrived(i) + extra[i][n])
    for i in range(n_b):
        remote(total[i].at[other], extra[i], x_send.at[i, 0], x_recv.at[i, 0], x_id).wait_recv()
        finish(i, total[i][xl] + extra[i][...])

    def along(src, d, j, k):
        n = index(d, j)
        return remote(hid.at[src, xl], hid.at[src, xl], ag_send.at[n], ag_recv.at[n], z_id(d, k))

    stores = []

    def store(src, part_, n):
        copy = pltpu.make_async_copy(hid.at[src, part_], out_hbm.at[src, part_], out_sem.at[n])
        copy.start()
        stores.append(copy)

    def across(src, n):
        return remote(hid.at[src, xl], hid.at[src, xl], agx_send.at[n], agx_recv.at[n], x_id)

    def spread(src, d, j):
        for k in range(STRIDE, 0, -1):
            if j + k <= hops[d]:
                go(along(src, d, j + k, k))

    last = nz - 1
    for d in (0, 1):
        spread(z, d, 0)
    go(across(z, last))
    store(z, xl, last)
    arrivals = [(j, d) for j in range(1, hops[0] + 1) for d in (0, 1) if j <= hops[d]]
    for j, d in arrivals:
        src = at_z(d, -j)
        along(src, d, j, 1).wait_recv()
        if j % STRIDE == 0:
            spread(src, d, j)
        go(across(src, index(d, j)))
        store(src, xl, index(d, j))

    def mirrored(src, n):
        remote(hid.at[src, xl], hid.at[src, other], agx_send.at[n], agx_recv.at[n], x_id).wait_recv()
        store(src, other, nz + n)

    mirrored(z, last)
    for j, d in arrivals:
        mirrored(at_z(d, -j), index(d, j))
    for copy in started:
        copy.wait_send()
    for copy in stores:
        copy.wait()


def local(nz, ny, nx, tokens, gate_weight, up_weight):
    rows_each, depth = tokens.shape
    columns = gate_weight.shape[1]
    tiles = B_TILES + A_TILES
    widths = tuple(LANE * t for t in tiles)
    n_b = len(B_TILES)
    n_s = len(tiles)
    steps = nz - 1
    f32, bf16 = jnp.float32, jnp.bfloat16
    dma = pltpu.SemaphoreType.DMA
    n_peers = nx * ny - 1
    lead = [(2,) if i < n_b else () for i in range(n_s)]
    scratch = [
        pltpu.VMEM((2 * nx * ny, rows_each, depth), bf16),
        pltpu.VMEM((depth, columns), bf16),
        pltpu.VMEM((depth, columns), bf16),
        pltpu.VMEM((nz, 2, 8, columns), bf16),
    ]
    scratch += [pltpu.VMEM((nz, 2, 8, 2 * w), f32) for w in widths]
    scratch += [pltpu.VMEM((steps, *lead[i], 8, 2 * w), f32) for i, w in enumerate(widths)]
    scratch += [pltpu.VMEM((8, 2 * w) if i < n_b else (nz, 8, 2 * w), f32) for i, w in enumerate(widths)]
    scratch += [pltpu.VMEM((2, 8, 2 * w), f32) for w in widths[:n_b]]
    scratch += [dma((3,)), dma((n_peers,)), dma((n_peers,)), dma((n_peers + 1,)), dma((n_peers + 1,))]
    scratch += [dma((n_s, steps)), dma((n_s, steps)), dma((n_s, nz)), dma((n_s, nz))]
    scratch += [dma((steps,)), dma((steps,)), dma((nz,)), dma((nz,)), dma((2 * nz,))]
    hidden = pl.pallas_call(
        functools.partial(kernel, nz, ny, nx, widths, n_b),
        out_shape=jax.ShapeDtypeStruct((nz, 2, 8, columns), bf16),
        in_specs=[pl.BlockSpec(memory_space=pl.ANY)] * 3,
        out_specs=pl.BlockSpec(memory_space=pl.ANY),
        scratch_shapes=scratch,
        compiler_params=pltpu.CompilerParams(
            collective_id=0, has_side_effects=True, vmem_limit_bytes=67_043_328
        ),
        name="swiglu",
    )(tokens, gate_weight, up_weight)
    return hidden.reshape(nz * 16, columns)


def solution(mesh):
    rows, cols = mesh.shape["row"], mesh.shape["col"]
    nx, ny = 2, rows // 4
    return jax.shard_map(
        functools.partial(local, cols // 2, ny, nx),
        mesh=mesh,
        in_specs=(P("row", "col"), P("col", "row"), P("col", "row")),
        out_specs=P(None, "row"),
        check_vma=False,
    )
```

time: 177 us -> 87.6 us (0.49)
  the two profiles are of different devices: /device:TPU:16 before, /device:TPU:2 now
where the time goes in v1:
time: 87.6 us; the launch traced here: 87.5 us
  Pallas kernels  85.3 us (97%)
  local copies, waits for them, and re-layouts  2.12 us (2%)
    pallas_call x1, Pallas kernels, local(): pl.pallas_call(functools.partial(kernel, nz, ny, nx, widths, n_b), out_sh...  85.3 us
    unnamed x1, local copies, waits for them, and re-layouts  2.12 us

profile of v1, /device:TPU:2, one launch (start us, length us, event | category | flops | bytes accessed | tf_op | source)
XLA Modules:
  0.0 87.5 jit_solution(14813680125720694296)
XLA Ops:
  0.0 85.3 %swiglu.1 = bf16[16,2,8,1664]{3,2,1,0:T(8,128)(2,1)} custom-call(bf16[16,512]{1,0:T(8,128)(2,1)} %tok_hbm.1, bf16[512,1664]{1,0:T(8,128)(2,1)} %gate_hbm.1, bf16[512,1664]{1,0:T(8,128)(2,1)} %up_hbm.1), custom_call_target="tpu_custom_call" | custom-call | tf_op jit(solution)/shard_map/swiglu/pallas_call | solution.py:252
  85.4 2.1 %copy.5 = bf16[256,1664]{1,0:T(8,128)(2,1)} copy(bf16[256,1664]{1,0:T(8,128)(2,1)} %bitcast.1) | data formatting | bytes 1703936

commit v2 on v1

v2 whole, which is shorter than its diff:
```python
import functools

import jax
import jax.numpy as jnp
from jax import lax
from jax.experimental import pallas as pl
from jax.experimental.pallas import tpu as pltpu
from jax.sharding import PartitionSpec as P

LANE = 128
B_TILES = (3, 2)
A_TILES = (4, 4)
STRIDE = 2


def kernel(nz, ny, nx, widths, n_b, tok_hbm, gate_hbm, up_hbm, hid, *scratch):
    scratch = list(scratch)
    take = scratch.pop
    tok, wg, wu = take(0), take(0), take(0)
    n_s = len(widths)
    part = [take(0) for _ in range(n_s)]
    slot = [take(0) for _ in range(n_s)]
    extra = [take(0) for _ in range(n_s)]
    total = [take(0) for _ in range(n_b)]
    load_sem, tok_send, tok_recv, pass_send, pass_recv = [take(0) for _ in range(5)]
    rs_send, rs_recv, x_send, x_recv = [take(0) for _ in range(4)]
    ag_send, ag_recv, agx_send, agx_recv = [take(0) for _ in range(4)]

    row, col = lax.axis_index("row"), lax.axis_index("col")
    core = lax.rem(row, 2)
    y = lax.rem(row // 2, ny)
    xh = row // (2 * ny)
    z = col // 2
    xl = lax.rem(col, 2)
    other = 1 - xl
    sign = (1 - 2 * core, 2 * core - 1)
    hops = (nz // 2, nz - 1 - nz // 2)

    def at_z(d, t):
        return lax.rem(z + sign[d] * t + 2 * nz, nz)

    def z_id(d, t):
        return {"col": at_z(d, t) * 2 + xl}

    def row_of(dx, dy):
        return (lax.rem(xh + dx + nx, nx) * ny + lax.rem(y + dy + ny, ny)) * 2 + core

    x_id = {"col": z * 2 + other}
    partner = {"row": row + 1 - 2 * core}

    def remote(src, dst, send, recv, device):
        return pltpu.make_async_remote_copy(
            src_ref=src, dst_ref=dst, send_sem=send, recv_sem=recv,
            device_id=device, device_id_type=pl.DeviceIdType.MESH,
        )

    loads = [
        pltpu.make_async_copy(tok_hbm, tok.at[row], load_sem.at[0]),
        pltpu.make_async_copy(gate_hbm, wg, load_sem.at[1]),
        pltpu.make_async_copy(up_hbm, wu, load_sem.at[2]),
    ]
    for copy in loads:
        copy.start()

    offsets = [(dx, dy) for dx in range(nx) for dy in range(ny) if dx or dy]
    peers = [{"row": row_of(dx, dy)} for dx, dy in offsets]
    greet = peers + [partner, x_id]
    near = sorted({(d, t) for d in (0, 1) for t in range(1, STRIDE + 1)})
    greet += [z_id(d, t) for d, t in near]
    barrier = pltpu.get_barrier_semaphore()
    for device in greet:
        pl.semaphore_signal(barrier, inc=1, device_id=device, device_id_type=pl.DeviceIdType.MESH)
    with jax.named_scope("greet"):
        pl.semaphore_wait(barrier, len(greet))

    with jax.named_scope("load"):
        loads[0].wait()
    for o, device in reversed(list(enumerate(peers))):
        remote(tok.at[row], tok.at[row], tok_send, tok_recv.at[o], device).start()
    remote(tok.at[row], tok.at[row], pass_send, pass_recv, partner).start()
    for o, (dx, dy) in enumerate(offsets):
        src = row_of(-dx, -dy)
        with jax.named_scope(f"tok{o}"):
            remote(tok.at[src], tok.at[src], tok_send, tok_recv.at[o], peers[o]).wait_recv()
        remote(tok.at[src], tok.at[src], pass_send, pass_recv, partner).start()
    all_passed = tok.at[pl.ds(0, len(peers) + 1)]
    with jax.named_scope("passed"):
        remote(all_passed, all_passed, pass_send, pass_recv, partner).wait_recv()
    with jax.named_scope("weights"):
        loads[1].wait()
        loads[2].wait()
    n_rows, rows_each, depth = tok.shape
    x = tok[...].reshape(n_rows * rows_each, depth)

    starts = [sum(widths[:i]) for i in range(n_s)]

    def multiply(i):
        w = widths[i]
        for half, ref in enumerate((wg, wu)):
            y_ = jnp.dot(x, ref[:, starts[i] : starts[i] + w], preferred_element_type=jnp.float32)
            part[i][:, :, :, half * w : (half + 1) * w] = y_.reshape(nz, 2, 8, w)

    order = [(d, t) for t in range(hops[0], 0, -1) for d in (0, 1) if t <= hops[d]] + [(0, 0)]
    place = {key: n for n, key in enumerate(order)}

    def index(d, t):
        return d * hops[0] + t - 1

    def rs(i, d, t, src):
        n = index(d, t)
        return remote(src, slot[i].at[n], rs_send.at[i], rs_recv.at[i, n], z_id(d, 1))

    def xs(i, n):
        d, t = order[n]
        return remote(part[i].at[at_z(d, t), other], extra[i].at[n], x_send.at[i], x_recv.at[i, n], x_id)

    def own(i, d, t):
        return part[i].at[at_z(d, t)] if i < n_b else part[i].at[at_z(d, t), xl]

    def step(i, d, t):
        ref = own(i, d, t)
        if i >= n_b:
            n = place[d, t]
            xs(i, n).wait_recv()
            ref[...] = ref[...] + extra[i][n]
        if t < hops[d]:
            n = index(d, t + 1)
            rs(i, d, t + 1, slot[i].at[n]).wait_recv()
            slot[i][n] = slot[i][n] + ref[...]
            ref = slot[i].at[n]
        rs(i, d, t, ref).start()

    for i in range(n_s):
        with jax.named_scope(f"mul{i}"):
            multiply(i)
        if i < n_b:
            for d in (0, 1):
                step(i, d, hops[d])
    for n in range(len(order)):
        for i in range(n_b, n_s):
            xs(i, n).start()
    for t in range(hops[0], 0, -1):
        for i in range(n_s):
            for d in (0, 1):
                if t > hops[d] or (i < n_b and t == hops[d]):
                    continue
                with jax.named_scope(f"rs{t}s{i}d{d}"):
                    step(i, d, t)

    def arrived(i):
        if hops[1]:
            ends = (0, 1)
        else:
            ends = (0,)
        for d in ends:
            rs(i, d, 1, slot[i].at[index(d, 1)]).wait_recv()
        value = slot[i][index(0, 1)]
        if hops[1]:
            value = value + slot[i][index(1, 1)]
        return value + own(i, 0, 0)[...]

    def finish(i, value):
        w = widths[i]
        gate, up = value[:, :w], value[:, w:]
        hid[z * 2 + xl, :, starts[i] : starts[i] + w] = (gate / (1.0 + jnp.exp(-gate)) * up).astype(jnp.bfloat16)

    for i in range(n_b):
      with jax.named_scope(f"tot{i}"):
        total[i][...] = arrived(i)
        remote(total[i].at[other], extra[i], x_send.at[i], x_recv.at[i, 0], x_id).start()
    for i in range(n_b, n_s):
        n = place[0, 0]
        with jax.named_scope(f"fin{i}"):
            xs(i, n).wait_recv()
            finish(i, arrived(i) + extra[i][n])
    for i in range(n_b):
        with jax.named_scope(f"fin{i}"):
            remote(total[i].at[other], extra[i], x_send.at[i], x_recv.at[i, 0], x_id).wait_recv()
            finish(i, total[i][xl] + extra[i][...])

    def along(src, d, j, k):
        ref = hid.at[src * 2 + xl]
        return remote(ref, ref, ag_send, ag_recv.at[index(d, j)], z_id(d, k))

    def across(src, side, n):
        ref = hid.at[src * 2 + side]
        return remote(ref, ref, agx_send, agx_recv.at[n], x_id)

    def spread(src, d, j):
        for k in range(STRIDE, 0, -1):
            if j + k <= hops[d]:
                along(src, d, j + k, k).start()

    last = nz - 1
    for d in (0, 1):
        spread(z, d, 0)
    across(z, xl, last).start()
    arrivals = [(j, d) for j in range(1, hops[0] + 1) for d in (0, 1) if j <= hops[d]]
    for j, d in arrivals:
        src = at_z(d, -j)
        with jax.named_scope(f"ag{j}d{d}"):
            along(src, d, j, 1).wait_recv()
        if j % STRIDE == 0:
            spread(src, d, j)
        across(src, xl, index(d, j)).start()
    with jax.named_scope("mir"):
        across(z, other, last).wait_recv()
    for j, d in arrivals:
        with jax.named_scope(f"mir{j}d{d}"):
            across(at_z(d, -j), other, index(d, j)).wait_recv()

    def sent(ref, sem):
        pltpu.make_async_copy(ref, ref, sem).wait()

    with jax.named_scope("sent"):
        sent(tok.at[pl.ds(0, len(peers))], tok_send)
        sent(all_passed, pass_send)
        for i in range(n_s):
            sent(slot[i], rs_send.at[i])
            sent(extra[i], x_send.at[i])
        sent(hid.at[pl.ds(0, nz - 1)], ag_send)
        sent(hid.at[pl.ds(0, nz)], agx_send)


def local(nz, ny, nx, tokens, gate_weight, up_weight):
    rows_each, depth = tokens.shape
    columns = gate_weight.shape[1]
    tiles = B_TILES + A_TILES
    widths = tuple(LANE * t for t in tiles)
    n_b = len(B_TILES)
    n_s = len(tiles)
    steps = nz - 1
    f32, bf16 = jnp.float32, jnp.bfloat16
    dma = pltpu.SemaphoreType.DMA
    n_peers = nx * ny - 1
    lead = [(2,) if i < n_b else () for i in range(n_s)]
    scratch = [
        pltpu.VMEM((2 * nx * ny, rows_each, depth), bf16),
        pltpu.VMEM((depth, columns), bf16),
        pltpu.VMEM((depth, columns), bf16),
    ]
    scratch += [pltpu.VMEM((nz, 2, 8, 2 * w), f32) for w in widths]
    scratch += [pltpu.VMEM((steps, *lead[i], 8, 2 * w), f32) for i, w in enumerate(widths)]
    scratch += [pltpu.VMEM((8, 2 * w) if i < n_b else (nz, 8, 2 * w), f32) for i, w in enumerate(widths)]
    scratch += [pltpu.VMEM((2, 8, 2 * w), f32) for w in widths[:n_b]]
    scratch += [dma((3,)), dma, dma((n_peers,)), dma, dma]
    scratch += [dma((n_s,)), dma((n_s, steps)), dma((n_s,)), dma((n_s, nz))]
    scratch += [dma, dma((steps,)), dma, dma((nz,))]
    hidden = pl.pallas_call(
        functools.partial(kernel, nz, ny, nx, widths, n_b),
        out_shape=pltpu.VMEM((2 * nz, 8, columns), bf16),
        in_specs=[pl.BlockSpec(memory_space=pl.ANY)] * 3,
        out_specs=pl.BlockSpec(memory_space=pltpu.VMEM),
        scratch_shapes=scratch,
        compiler_params=pltpu.CompilerParams(
            collective_id=0, has_side_effects=True, vmem_limit_bytes=66_187_264
        ),
        name="swiglu",
    )(tokens, gate_weight, up_weight)
    return hidden.reshape(nz * 16, columns)


def solution(mesh):
    rows, cols = mesh.shape["row"], mesh.shape["col"]
    nx, ny = 2, rows // 4
    return jax.shard_map(
        functools.partial(local, cols // 2, ny, nx),
        mesh=mesh,
        in_specs=(P("row", "col"), P("col", "row"), P("col", "row")),
        out_specs=P(None, "row"),
        check_vma=False,
    )
```

time: 87.6 us -> 74.2 us (0.85)
  Pallas kernels: 85.3 us -> 73.2 us
  local copies, waits for them, and re-layouts: 2.12 us -> 0.9 us
    pallas_call x1, Pallas kernels: 85.3 us -> 73.2 us  [local(): pl.pallas_call(functools.partial(kernel, nz, ny, nx, widths, n_b), out_sh...]
    unnamed x1, local copies, waits for them, and re-layouts: 2.12 us -> 0.9 us
where the time goes in v2:
time: 74.2 us; the launch traced here: 74.1 us
  Pallas kernels  73.2 us (99%)
  local copies, waits for them, and re-layouts  0.9 us (1%)
    pallas_call x1, Pallas kernels, local(): pl.pallas_call(functools.partial(kernel, nz, ny, nx, widths, n_b), out_sh...  73.2 us

profile of v2, /device:TPU:2, one launch (start us, length us, event | category | flops | bytes accessed | tf_op | source)
XLA Modules:
  0.0 74.1 jit_solution(16231834954343343526)
XLA Ops:
  0.0 73.2 %swiglu.1 = bf16[32,8,1664]{2,1,0:T(8,128)(2,1)S(1)} custom-call(bf16[16,512]{1,0:T(8,128)(2,1)} %tok_hbm.1, bf16[512,1664]{1,0:T(8,128)(2,1)} %gate_hbm.1, bf16[512,1664]{1,0:T(8,128)(2,1)} %up_hbm.1), custom_call_target="tpu_custom_call" | custom-call | tf_op jit(solution)/shard_map/swiglu/pallas_call | solution.py:249
  73.2 0.9 %copy.5 = bf16[256,1664]{1,0:T(8,128)(2,1)} copy(bf16[256,1664]{1,0:T(8,128)(2,1)S(1)} %bitcast.1) | data formatting | bytes 1703936
